TPU v7x, 32 devices: a whole 2x2x4 slice. The times are simulated.
32 devices in a mesh: dp: 8 (over z, y), owner: 4 (over x, core).
Axes of the slice: x: 2, y: 2, z: 4, core: 2. Of those that a mesh axis runs over, the one named last changes fastest.
Arguments:
- grads: float32 [8, 32, 512, 128], P('dp', None, 'owner'), may hold values from -21 to 21
- momentum: float32 [64, 512, 128], P('dp', 'owner'), may hold values from -30 to 30
- slot_matrix: int32 [64], replicated, may hold values from -1 to 31, as said below
Outputs:
- updates: bfloat16 [32, 512, 128], P(None, 'owner')
- momentum_out: float32 [64, 512, 128], P('dp', 'owner')
Inputs may be any that keep to these rules, and one draw needn't show every extreme that they name: `slot_matrix`: entry s names the block held by slot s, or is -1 if slot s is empty; slots s with s // 8 == g belong to the owner group at index g of dp. Every one of the 32 blocks is held by exactly one slot, and some group, drawn from the seed, has all 8 slots filled.
All inputs are finite; a program needn't handle non-finite values.
Results may differ from a plain program's by a relative error of at most 0.038.
Values may be sent and summed in bfloat16 or wider, within the bound.
A program may use at most 64 MiB of HBM per device.

v0:
```python
import functools
import math

import jax
import jax.numpy as jnp
from jax import lax
from jax.experimental import pallas as pl
from jax.experimental.pallas import tpu as pltpu
from jax.sharding import PartitionSpec as P

ITERS = 5

momentum_rate = 0.95
epsilon_norm = 1e-07
first_coef = 3.4445
third_coef = -4.775
fifth_coef = 2.0315

MESH = pl.DeviceIdType.MESH
F32 = jnp.float32
BF16 = jnp.bfloat16


def normalized(x):
    norm = jnp.sqrt(jnp.sum(x * x, axis=(0, 1), keepdims=True)) + epsilon_norm
    return (x / norm).astype(BF16)


def sweep(iterate):
    gram = lax.dot_general(
        iterate, iterate, (((0,), (0,)), ((), ())), preferred_element_type=F32
    ).astype(BF16)
    square = jnp.dot(gram, gram, preferred_element_type=F32)
    poly = (third_coef * gram.astype(F32) + fifth_coef * square).astype(BF16)
    return first_coef * iterate.astype(F32) + jnp.dot(iterate, poly, preferred_element_type=F32)


def kernel(
    n_dp, n_ow, per, workers,
    slots_ref, grads_ref, mom_ref, upd_ref, momout_ref,
    ypack, yrecv, zsend, zrecv, own, held, orecv, work, ubuf, every, ysel, yselrecv,
    ys, yr, zs, zr, os_, or_, ms, mr, qs, qr, us, ur, vs, vr, ws, wr, bs, br,
):
    n_z = n_dp // 2
    mats = grads_ref.shape[0]
    nb = mats // n_dp
    n_slots = mom_ref.shape[0]
    dp = lax.axis_index("dp")
    ow = lax.axis_index("owner")
    z = lax.div(dp, 2)
    y = lax.rem(dp, 2)
    other = 2 * z + 1 - y

    def up(t):
        return lax.rem(z + 1 + t, n_z)

    def down(t):
        return lax.rem(z - 1 - t + 2 * n_z, n_z)

    def owner_at(t):
        return lax.rem(ow + t, n_ow)

    def owner_from(t):
        return lax.rem(ow - t + n_ow, n_ow)

    def remote(src, dst, send, recv, to):
        return pltpu.make_async_remote_copy(
            src_ref=src, dst_ref=dst, send_sem=send, recv_sem=recv,
            device_id=to, device_id_type=MESH,
        )

    barrier = pltpu.get_barrier_semaphore()
    pl.semaphore_signal(barrier, inc=1, device_id=(other, ow), device_id_type=MESH)
    for t in range(n_z - 1):
        pl.semaphore_signal(barrier, inc=1, device_id=(2 * up(t) + y, ow), device_id_type=MESH)
    for t in range(1, n_ow):
        pl.semaphore_signal(barrier, inc=1, device_id=(dp, owner_at(t)), device_id_type=MESH)

    held_slots = [slots_ref[dp * n_slots + k] for k in range(n_slots)]

    def partial(m):
        place = jnp.int32(0)
        weight = F32(0.0)
        for k in range(n_slots):
            hit = held_slots[k] == m
            place = jnp.where(hit, k, place)
            weight = jnp.where(hit, F32(momentum_rate), weight)
        return grads_ref[m] + weight * mom_ref[place]

    y_copies = []
    for t in range(n_z):
        def pack(j, carry, t=t):
            ypack[t, j] = partial((2 * up(t) + 1 - y) * nb + j).astype(BF16)
            return carry
        lax.fori_loop(0, nb, pack, 0)
        if t == 0:
            pl.semaphore_wait(barrier, 1 + (n_z - 1) + (n_ow - 1))
        copy = remote(ypack.at[t], yrecv.at[t], ys.at[t], yr.at[t], (other, ow))
        copy.start()
        y_copies.append(copy)

    z_copies = []
    for t in range(n_z):
        y_copies[t].wait_recv()
        def add(j, carry, t=t):
            value = partial((2 * up(t) + y) * nb + j) + yrecv[t, j].astype(F32)
            if t < n_z - 1:
                zsend[t, j] = value.astype(BF16)
            else:
                own[j] = value
            return carry
        lax.fori_loop(0, nb, add, 0)
        if t < n_z - 1:
            copy = remote(zsend.at[t], zrecv.at[t], zs.at[t], zr.at[t], (2 * up(t) + y, ow))
            copy.start()
            z_copies.append(copy)

    for copy in z_copies:
        copy.wait_recv()

    mine = pl.ds(z * nb, nb)

    def total(j, carry):
        value = own[j]
        for t in range(n_z - 1):
            value = value + zrecv[t, j].astype(F32)
        held[z * nb + j] = value.astype(BF16)
        return carry
    lax.fori_loop(0, nb, total, 0)

    def when_worker(index, fn):
        if workers == n_ow:
            fn()
        else:
            pl.when(index < workers)(fn)

    def share(j):
        return pl.ds(j * per, per)

    o_copies = []
    for t in range(1, n_ow):
        j = owner_at(t)
        copy = remote(
            held.at[pl.ds(z * nb + j * per, per)], orecv.at[ow],
            os_.at[t - 1], or_.at[t - 1], (dp, j),
        )
        when_worker(j, copy.start)
        o_copies.append(copy)
    flows = ((1, z < n_z - 1), (-1, z > 0))

    def within(index):
        return jnp.logical_and(index >= 0, index < n_z)

    def leg(f, k, item, region, buf, send, recv):
        step, open_ahead = flows[f]
        chunk = z - step * k
        where = region(chunk)
        to = jnp.clip(z + step, 0, n_z - 1)
        copy = remote(
            buf.at[where], buf.at[where], send.at[f, k, item], recv.at[f, k, item],
            (2 * to + y, ow),
        )
        sends = jnp.logical_and(open_ahead, within(chunk))
        takes = within(chunk - step)
        return copy, sends, takes

    pending = []

    def launch(legs, k, item):
        for f in range(2):
            copy, sends, _ = legs(f, k, item)
            pl.when(sends)(copy.start)
            pending.append((copy, sends))

    def arrive(legs, k, item):
        for f in range(2):
            copy, _, takes = legs(f, k, item)
            pl.when(takes)(copy.wait_recv)

    half = nb // 2
    parts = ((0, half), (half, nb - half))

    def m_legs(f, k, item):
        first, count = parts[item]
        return leg(f, k, item, lambda c: pl.ds(c * nb + first, count), held, ms, mr)

    def m_pass(k, item):
        if k > 0:
            arrive(m_legs, k - 1, item)
        if k < n_z - 1:
            launch(m_legs, k, item)

    m_pass(0, 0)
    m_pass(0, 1)

    def keep_own():
        orecv[ow] = held[pl.ds(z * nb + ow * per, per)]
    when_worker(ow, keep_own)

    def begin():
        for copy in o_copies:
            copy.wait_recv()
        for p in range(per):
            pieces = [orecv[o, p].astype(F32) for o in range(n_ow)]
            work[p] = normalized(jnp.concatenate(pieces, axis=0))

    def sweeps(count):
        def run():
            for p in range(per):
                iterate = work[p]
                for _ in range(count):
                    iterate = sweep(iterate).astype(BF16)
                work[p] = iterate
        return run

    def end():
        for p in range(per):
            advanced = sweep(work[p])
            update = (math.sqrt(advanced.shape[0]) * advanced).astype(BF16)
            rows = update.shape[0] // n_ow
            for o in range(n_ow):
                ubuf[o, p] = update[o * rows:(o + 1) * rows]

    before = (ITERS - 1) // 2
    when_worker(ow, begin)
    m_pass(1, 0)
    when_worker(ow, sweeps(before))
    m_pass(1, 1)
    when_worker(ow, sweeps(ITERS - 1 - before))
    when_worker(ow, end)

    home = pl.ds(dp * nb + ow * per, per)
    u_copies = []
    for t in range(1, n_ow):
        j = owner_at(t)
        copy = remote(ubuf.at[j], every.at[home], us.at[t - 1], ur.at[t - 1], (dp, j))
        when_worker(ow, copy.start)
        u_copies.append(copy)

    def keep_update():
        every[home] = ubuf[ow]
    when_worker(ow, keep_update)

    for k in range(2, n_z - 1):
        for item in range(2):
            m_pass(k, item)

    for t in range(1, n_ow):
        when_worker(owner_from(t), u_copies[t - 1].wait_recv)

    def v_region(item):
        first, count = parts[0] if item == 0 else parts[1]
        side = 1 - y if item == 2 else y
        return lambda c: pl.ds((2 * c + side) * nb + first, count)

    def v_legs(f, k, item):
        return leg(f, k, item, v_region(item), every, vs, vr)

    b_own = every.at[v_region(1)(z)]
    b_copy = remote(b_own, b_own, bs, br, (other, ow))
    b_copy.start()
    launch(v_legs, 0, 0)
    launch(v_legs, 0, 1)

    def across(chunk, sem):
        piece = every.at[v_region(0)(chunk)]
        return remote(piece, piece, ws.at[sem], wr.at[sem], (other, ow))

    a_copies = [(across(z, 2 * (n_z - 1)), None)]
    a_copies[0][0].start()

    m_pass(n_z - 1, 0)
    m_pass(n_z - 1, 1)

    def place_of(m):
        m = jnp.maximum(m, 0)
        return lax.div(m, 2 * nb) * nb + lax.rem(m, nb)

    def pick(k, carry):
        ysel[k] = held[place_of(slots_ref[other * n_slots + k])]
        return carry
    lax.fori_loop(0, n_slots, pick, 0)
    q_copy = remote(ysel, yselrecv, qs, qr, (other, ow))
    q_copy.start()

    b_copy.wait_recv()
    launch(v_legs, 0, 2)

    def v_pass(k):
        for item in range(3):
            arrive(v_legs, k - 1, item)
            if k < n_z - 1:
                launch(v_legs, k, item)
            if item == 0:
                for f in range(2):
                    chunk = z - flows[f][0] * k
                    copy = across(chunk, 2 * (k - 1) + f)
                    pl.when(within(chunk))(copy.start)
                    a_copies.append((copy, within(chunk)))

    for k in range(1, n_z - 1):
        v_pass(k)

    q_copy.wait_recv()

    def renew(k, carry):
        m = slots_ref[dp * n_slots + k]
        side = lax.rem(lax.div(jnp.maximum(m, 0), nb), 2)
        local = jnp.where(side == y, F32(1.0), F32(0.0))
        present = jnp.where(m >= 0, F32(1.0), F32(0.0))
        near = held[place_of(m)].astype(F32)
        far = yselrecv[k].astype(F32)
        summed = present * (local * near + (1.0 - local) * far)
        momout_ref[k] = summed + (1.0 - present) * (F32(momentum_rate) * mom_ref[k])
        return carry
    lax.fori_loop(0, n_slots, renew, 0)

    v_pass(n_z - 1)
    for copy, there in a_copies:
        if there is None:
            copy.wait_recv()
        else:
            pl.when(there)(copy.wait_recv)
    upd_ref[...] = every[...]

    for copy in y_copies + z_copies + [q_copy, b_copy, a_copies[0][0]]:
        copy.wait_send()
    for copy, sent in pending + a_copies[1:]:
        pl.when(sent)(copy.wait_send)
    for t in range(1, n_ow):
        when_worker(owner_at(t), o_copies[t - 1].wait_send)
        when_worker(ow, u_copies[t - 1].wait_send)


def local(n_dp, n_ow, grads, momentum, slot_matrix):
    mats, rows, cols = grads.shape[1:]
    n_slots = momentum.shape[0]
    nb = mats // n_dp
    n_z = n_dp // 2
    workers = min(nb, n_ow)
    per = nb // workers
    block = (rows, cols)
    vmem = pl.BlockSpec(memory_space=pltpu.VMEM)
    dma = pltpu.SemaphoreType.DMA
    hops = n_z - 1
    counts = (
        (n_z,), (hops,), (n_ow - 1,), (2, hops, 2), (), (n_ow - 1,), (2, hops, 3), (2 * hops + 1,), ()
    )
    sems = []
    for count in counts:
        sems += [dma(count) if count else dma] * 2
    updates, renewed = pl.pallas_call(
        functools.partial(kernel, n_dp, n_ow, per, workers),
        out_shape=(
            jax.ShapeDtypeStruct((mats,) + block, BF16),
            jax.ShapeDtypeStruct(momentum.shape, F32),
        ),
        in_specs=[pl.BlockSpec(memory_space=pltpu.SMEM), vmem, vmem],
        out_specs=(vmem, vmem),
        scratch_shapes=[
            pltpu.VMEM((n_z, nb) + block, BF16),
            pltpu.VMEM((n_z, nb) + block, BF16),
            pltpu.VMEM((n_z - 1, nb) + block, BF16),
            pltpu.VMEM((n_z - 1, nb) + block, BF16),
            pltpu.VMEM((nb,) + block, F32),
            pltpu.VMEM((n_z * nb,) + block, BF16),
            pltpu.VMEM((n_ow, per) + block, BF16),
            pltpu.VMEM((per, n_ow * rows, cols), BF16),
            pltpu.VMEM((n_ow, per) + block, BF16),
            pltpu.VMEM((mats,) + block, BF16),
            pltpu.VMEM((n_slots,) + block, BF16),
            pltpu.VMEM((n_slots,) + block, BF16),
        ] + sems,
        compiler_params=pltpu.CompilerParams(collective_id=0, has_side_effects=True),
    )(slot_matrix, grads[0], momentum)
    return updates, renewed


def solution(mesh):
    return jax.shard_map(
        functools.partial(local, mesh.shape["dp"], mesh.shape["owner"]),
        mesh=mesh,
        in_specs=(P("dp", None, "owner", None), P("dp", "owner", None), P()),
        out_specs=(P(None, "owner", None), P("dp", "owner", None)),
        check_vma=False,
    )
```

profile of v0, /device:TPU:0, one launch (start us, length us, event | category | flops | bytes accessed | tf_op | source)
XLA Modules:
  0.0 56.9 jit_solution(11888441239685943787)
XLA Ops:
  0.6 53.1 %shard_map.50 = (bf16[32,128,128]{2,1,0:T(8,128)(2,1)}, f32[8,128,128]{2,1,0:T(8,128)}) custom-call(s32[64]{0:T(128)} %slots_ref.1, f32[32,128,128]{2,1,0:T(8,128)} %bitcast.1, f32[8,128,128]{2,1,0:T(8,128)} %mom_ref.1), custom_call_target="tpu_custom_call" | custom-call | tf_op jit(solution)/shard_map/pallas_call | solution.py:352
  53.7 0.0 copy-start
  53.7 2.4 %copy.7 = bf16[32,128,128]{2,1,0:T(8,128)(2,1)} copy(bf16[32,128,128]{2,1,0:T(8,128)(2,1)} %get-tuple-element.4) | data formatting | bytes 2097152
  56.1 0.0 copy-done
  56.1 0.8 %copy.8 = f32[8,128,128]{2,1,0:T(8,128)} copy(f32[8,128,128]{2,1,0:T(8,128)S(1)} %copy-done) | data formatting | bytes 1048576
Async XLA Ops:
  53.7 2.4 %copy-start = (f32[8,128,128]{2,1,0:T(8,128)S(1)}, f32[8,128,128]{2,1,0:T(8,128)}, u32[]{:S(2)}) copy-start(f32[8,128,128]{2,1,0:T(8,128)} %get-tuple-element.5) | copy-start | bytes 1572868
where the time goes:
time: 57 us; the launch traced here: 56.9 us
  Pallas kernels  53.1 us (93%)
  local copies, waits for them, and re-layouts  3.16 us (6%)
  between operations  0.65 us (1%)
    pallas_call x1, Pallas kernels, local(): pl.pallas_call(functools.partial(kernel, n_dp, n_ow, per, workers), out_s...  53.1 us
    unnamed x4, local copies, waits for them, and re-layouts  3.16 us

commit v1 on v0

v1 whole, which is shorter than its diff:
```python
import functools
import math

import jax
import jax.numpy as jnp
from jax import lax
from jax.experimental import pallas as pl
from jax.experimental.pallas import tpu as pltpu
from jax.sharding import PartitionSpec as P

ITERS = 5

momentum_rate = 0.95
epsilon_norm = 1e-07
first_coef = 3.4445
third_coef = -4.775
fifth_coef = 2.0315

MESH = pl.DeviceIdType.MESH
F32 = jnp.float32
BF16 = jnp.bfloat16


def low_bit(d):
    return (d & -d).bit_length() - 1


def poly_of(iterate):
    gram = lax.dot_general(
        iterate, iterate, (((0,), (0,)), ((), ())), preferred_element_type=F32
    ).astype(BF16)
    square = jnp.dot(gram, gram, preferred_element_type=F32)
    return (third_coef * gram.astype(F32) + fifth_coef * square).astype(BF16)


def kernel(
    n_dp, n_ow, per, workers, pieces,
    slots_ref, grads_ref, mom_ref, upd_ref, momout_ref,
    ypack, yrecv, zsend, zrecv, held, orecv, work, scale_ref, pall,
    ys, yr, zs, zr, os_, or_, ms, mr, as_, ar, pzs, pzr, pys, pyr, pxs, pxr, pcs, pcr,
):
    n_z = n_dp // 2
    n_x = n_ow // 2
    bits = n_z.bit_length() - 1
    mats = grads_ref.shape[0]
    rows = grads_ref.shape[1]
    cols = grads_ref.shape[2]
    full = n_ow * rows
    nb = mats // n_dp
    each = nb // pieces
    n_slots = mom_ref.shape[0]
    dp = lax.axis_index("dp")
    ow = lax.axis_index("owner")
    z = lax.div(dp, 2)
    y = lax.rem(dp, 2)
    x = lax.div(ow, 2)
    core = lax.rem(ow, 2)
    other = 2 * z + 1 - y
    sibling = 2 * x + 1 - core

    def flip(d):
        out = z
        for i in range(bits):
            if (d >> i) & 1:
                out = out + (1 << i) * (1 - 2 * lax.rem(lax.div(z, 1 << i), 2))
        return out

    def peer(i):
        return 2 * flip(1 << i) + y

    def member(d, s):
        return 2 * flip(d) + (y if s == 0 else 1 - y)

    def owner_at(t):
        return lax.rem(ow + t, n_ow)

    def owner_from(t):
        return lax.rem(ow - t + n_ow, n_ow)

    def remote(src, dst, send, recv, to):
        return pltpu.make_async_remote_copy(
            src_ref=src, dst_ref=dst, send_sem=send, recv_sem=recv,
            device_id=to, device_id_type=MESH,
        )

    sent = []

    def launch(copy, lane=None):
        when_worker(lane, copy.start)
        sent.append((copy, lane))
        return copy

    def when_worker(lane, fn):
        if lane is None or workers == n_ow:
            fn()
        else:
            pl.when(lane < workers)(fn)

    barrier = pltpu.get_barrier_semaphore()
    pl.semaphore_signal(barrier, inc=1, device_id=(other, ow), device_id_type=MESH)
    for i in range(bits):
        pl.semaphore_signal(barrier, inc=1, device_id=(peer(i), ow), device_id_type=MESH)
    for t in range(1, n_ow):
        pl.semaphore_signal(barrier, inc=1, device_id=(dp, owner_at(t)), device_id_type=MESH)

    held_slots = [slots_ref[dp * n_slots + k] for k in range(n_slots)]

    def partial(m):
        place = jnp.int32(0)
        weight = F32(0.0)
        for k in range(n_slots):
            hit = held_slots[k] == m
            place = jnp.where(hit, k, place)
            weight = jnp.where(hit, F32(momentum_rate), weight)
        return grads_ref[m] + weight * mom_ref[place]

    y_copies = {}
    for d in reversed(range(n_z)):
        for q in range(pieces):
            def pack(j, carry, d=d, q=q):
                b = q * each + j
                ypack[d, b] = partial(member(d, 1) * nb + b).astype(BF16)
                return carry
            lax.fori_loop(0, each, pack, 0)
            if d == n_z - 1 and q == 0:
                pl.semaphore_wait(barrier, 1 + bits + (n_ow - 1))
            part = pl.ds(q * each, each)
            y_copies[d, q] = launch(remote(
                ypack.at[d, part], yrecv.at[d, part], ys.at[d, q], yr.at[d, q], (other, ow)))

    def z_copy(d, q):
        part = pl.ds(q * each, each)
        return remote(
            zsend.at[d - 1, part], zrecv.at[d - 1, part], zs.at[d - 1, q], zr.at[d - 1, q],
            (peer(low_bit(d)), ow))

    for d in reversed(range(n_z)):
        steps = low_bit(d) if d else bits
        for q in range(pieces):
            y_copies[d, q].wait_recv()
            for i in range(steps):
                z_copy(d + (1 << i), q).wait_recv()

            def add(j, carry, d=d, q=q, steps=steps):
                b = q * each + j
                value = partial(member(d, 0) * nb + b) + yrecv[d, b].astype(F32)
                for i in range(steps):
                    value = value + zrecv[d + (1 << i) - 1, b].astype(F32)
                if d:
                    zsend[d - 1, b] = value.astype(BF16)
                else:
                    held[dp * nb + b] = value.astype(BF16)
                return carry
            lax.fori_loop(0, each, add, 0)
            if d:
                launch(z_copy(d, q))

    o_copies = []
    for t in range(1, n_ow):
        j = owner_at(t)
        copy = remote(
            held.at[pl.ds(dp * nb + j * per, per)], orecv.at[ow],
            os_.at[t - 1], or_.at[t - 1], (dp, j))
        launch(copy, j)
        o_copies.append(copy)

    def m_copy(d, q):
        where = pl.ds(member(d & (d - 1), 0) * nb + q * each, each)
        there = held.at[where]
        return remote(there, there, ms.at[d - 1, q], mr.at[d - 1, q], (peer(low_bit(d)), ow))

    def m_arrival(d, q):
        where = pl.ds(member(d, 0) * nb + q * each, each)
        here = held.at[where]
        return remote(here, here, ms.at[d - 1, q], mr.at[d - 1, q], (peer(low_bit(d)), ow))

    def across(d, q, s=0):
        where = pl.ds(member(d, s) * nb + q * each, each)
        piece = held.at[where]
        return remote(piece, piece, as_.at[d, q], ar.at[d, q], (other, ow))

    def m_spread(d, q):
        for i in reversed(range(low_bit(d) if d else bits)):
            launch(m_copy(d + (1 << i), q))
        launch(across(d, q))

    def m_pass(d):
        for q in range(pieces):
            m_arrival(d, q).wait_recv()
            m_spread(d, q)

    for q in range(pieces):
        m_spread(0, q)

    def begin():
        orecv[ow] = held[pl.ds(dp * nb + ow * per, per)]
        for copy in o_copies:
            copy.wait_recv()
        for p in range(per):
            block = jnp.concatenate([orecv[o, p].astype(F32) for o in range(n_ow)], axis=0)
            norm = jnp.sqrt(jnp.sum(block * block, axis=(0, 1), keepdims=True)) + epsilon_norm
            iterate = (block / norm).astype(BF16)
            scale_ref[p] = jnp.broadcast_to(math.sqrt(full) / norm, scale_ref.shape[1:])
            poly = poly_of(iterate)
            advanced = first_coef * iterate.astype(F32) + jnp.dot(
                iterate, poly, preferred_element_type=F32)
            work[p, pl.ds(0, full)] = advanced.astype(BF16)
            at_row = lax.broadcasted_iota(jnp.int32, (cols, cols), 0)
            at_col = lax.broadcasted_iota(jnp.int32, (cols, cols), 1)
            eye = jnp.where(at_row == at_col, F32(first_coef), F32(0.0))
            work[p, pl.ds(full, cols)] = (eye + poly.astype(F32)).astype(BF16)

    def sweeps(count):
        def run():
            for p in range(per):
                both = work[p]
                for _ in range(count):
                    poly = poly_of(both[:full])
                    both = (first_coef * both.astype(F32) + jnp.dot(
                        both, poly, preferred_element_type=F32)).astype(BF16)
                work[p] = both
        return run

    def end():
        for p in range(per):
            poly = poly_of(work[p, pl.ds(0, full)])
            factor = work[p, pl.ds(full, cols)]
            last = first_coef * factor.astype(F32) + jnp.dot(
                factor, poly, preferred_element_type=F32)
            pall[dp * nb + ow * per + p] = (scale_ref[p, 0:1] * last).astype(BF16)

    when_worker(ow, begin)
    when_worker(ow, sweeps(ITERS - 2))
    when_worker(ow, end)

    def unit(d, s, lane):
        return pall.at[pl.ds(member(d, s) * nb + lane * per, per)]

    def lane_from(t):
        return 2 * lax.rem(x - t + n_x, n_x) + core

    def lane_at(t):
        return 2 * lax.rem(x + t, n_x) + core

    def twin_from(t):
        return 2 * lax.rem(x - t + n_x, n_x) + 1 - core

    def pz_copy(d):
        there = unit(d & (d - 1), 0, ow)
        return remote(there, there, pzs.at[d - 1], pzr.at[d - 1], (peer(low_bit(d)), ow))

    def py_copy(d):
        there = unit(d, 0, ow)
        return remote(there, there, pys.at[d], pyr.at[d], (other, ow))

    def px_copy(d, s, t):
        there = unit(d, s, ow)
        return remote(there, there, pxs.at[t - 1, d, s], pxr.at[t - 1, d, s], (dp, lane_at(t)))

    def px_arrival(d, s, t):
        here = unit(d, s, lane_from(t))
        return remote(here, here, pxs.at[t - 1, d, s], pxr.at[t - 1, d, s], (dp, lane_at(t)))

    def pc_copy(d, s, t):
        there = unit(d, s, lane_from(t))
        return remote(there, there, pcs.at[t, d, s], pcr.at[t, d, s], (dp, sibling))

    def pc_arrival(d, s, t):
        here = unit(d, s, twin_from(t))
        return remote(here, here, pcs.at[t, d, s], pcr.at[t, d, s], (dp, sibling))

    def emit(d, s):
        for t in range(1, n_x):
            launch(px_copy(d, s, t), ow)
        launch(pc_copy(d, s, 0), ow)

    def p_spread(d):
        for i in reversed(range(low_bit(d) if d else bits)):
            launch(pz_copy(d + (1 << i)), ow)
        launch(py_copy(d), ow)
        emit(d, 0)

    def arrive_x(d, s):
        for t in range(1, n_x):
            lane = lane_from(t)
            when_worker(lane, px_arrival(d, s, t).wait_recv)
            launch(pc_copy(d, s, t), lane)

    def arrive_c(d, s):
        for t in range(n_x):
            when_worker(twin_from(t), pc_arrival(d, s, t).wait_recv)

    def form(d, s):
        first = member(d, s) * nb
        for b in range(nb):
            upd_ref[first + b] = jnp.dot(
                held[first + b], pall[first + b], preferred_element_type=F32).astype(BF16)

    def pz_arrival(d):
        here = unit(d, 0, ow)
        return remote(here, here, pzs.at[d - 1], pzr.at[d - 1], (peer(low_bit(d)), ow))

    def py_arrival(d):
        here = unit(d, 1, ow)
        return remote(here, here, pys.at[d], pyr.at[d], (other, ow))

    def renew():
        def one(k, carry):
            m = slots_ref[dp * n_slots + k]
            present = jnp.where(m >= 0, F32(1.0), F32(0.0))
            momout_ref[k] = present * held[jnp.maximum(m, 0)].astype(F32) + (
                1.0 - present) * (F32(momentum_rate) * mom_ref[k])
            return carry
        lax.fori_loop(0, n_slots, one, 0)

    order = [(0, 0), (0, 1)]
    for d in range(1, n_z):
        order.append((d, 0))
        if d > 1:
            order.append((d - 1, 1))
    order.append((n_z - 1, 1))
    lag_x, lag_c = 2, 4

    p_spread(0)
    for d in range(1, n_z - 1):
        m_pass(d)
    for i in range(len(order) + lag_c):
        if i < len(order):
            d, s = order[i]
            if s:
                when_worker(ow, py_arrival(d).wait_recv)
                emit(d, 1)
            elif d:
                when_worker(ow, pz_arrival(d).wait_recv)
                p_spread(d)
            if (d, s) == (n_z - 1, 0):
                m_pass(d)
        if 0 <= i - lag_x < len(order):
            arrive_x(*order[i - lag_x])
        if 0 <= i - lag_c < len(order):
            d, s = order[i - lag_c]
            arrive_c(d, s)
            if s:
                for q in range(pieces):
                    across(d, q, 1).wait_recv()
            form(d, s)
    renew()

    for copy, lane in sent:
        when_worker(lane, copy.wait_send)


def local(n_dp, n_ow, grads, momentum, slot_matrix):
    mats, rows, cols = grads.shape[1:]
    n_slots = momentum.shape[0]
    nb = mats // n_dp
    n_z = n_dp // 2
    n_x = n_ow // 2
    workers = min(nb, n_ow)
    per = nb // workers
    pieces = max(1, min(nb, 4 * nb // n_z))
    block = (rows, cols)
    vmem = pl.BlockSpec(memory_space=pltpu.VMEM)
    dma = pltpu.SemaphoreType.DMA
    hops = n_z - 1
    counts = (
        (n_z, pieces), (hops, pieces), (n_ow - 1,), (hops, pieces), (n_z, pieces),
        (hops,), (n_z,), (n_x - 1, n_z, 2), (n_x, n_z, 2),
    )
    sems = []
    for count in counts:
        sems += [dma(count)] * 2
    updates, renewed = pl.pallas_call(
        functools.partial(kernel, n_dp, n_ow, per, workers, pieces),
        out_shape=(
            jax.ShapeDtypeStruct((mats,) + block, BF16),
            jax.ShapeDtypeStruct(momentum.shape, F32),
        ),
        in_specs=[pl.BlockSpec(memory_space=pltpu.SMEM), vmem, vmem],
        out_specs=(vmem, vmem),
        scratch_shapes=[
            pltpu.VMEM((n_z, nb) + block, BF16),
            pltpu.VMEM((n_z, nb) + block, BF16),
            pltpu.VMEM((hops, nb) + block, BF16),
            pltpu.VMEM((hops, nb) + block, BF16),
            pltpu.VMEM((mats,) + block, BF16),
            pltpu.VMEM((n_ow, per) + block, BF16),
            pltpu.VMEM((per, n_ow * rows + cols, cols), BF16),
            pltpu.VMEM((per, 8, cols), F32),
            pltpu.VMEM((mats, cols, cols), BF16),
        ] + sems,
        compiler_params=pltpu.CompilerParams(collective_id=0, has_side_effects=True),
    )(slot_matrix, grads[0], momentum)
    return updates, renewed


def solution(mesh):
    return jax.shard_map(
        functools.partial(local, mesh.shape["dp"], mesh.shape["owner"]),
        mesh=mesh,
        in_specs=(P("dp", None, "owner", None), P("dp", "owner", None), P()),
        out_specs=(P(None, "owner", None), P("dp", "owner", None)),
        check_vma=False,
    )
```

time: 57 us -> 51.7 us (0.907)
  Pallas kernels: 53.1 us -> 47.3 us
    pallas_call x1, Pallas kernels: 53.1 us -> 47.3 us  [local(): pl.pallas_call(functools.partial(kernel, n_dp, n_ow, per, workers, pieces...]
where the time goes in v1:
time: 51.7 us; the launch traced here: 51.2 us
  Pallas kernels  47.3 us (91%)
  local copies, waits for them, and re-layouts  3.16 us (6%)
  between operations  0.65 us (1%)
    pallas_call x1, Pallas kernels, local(): pl.pallas_call(functools.partial(kernel, n_dp, n_ow, per, workers, pieces...  47.3 us
    unnamed x4, local copies, waits for them, and re-layouts  3.16 us

profile of v1, /device:TPU:0, one launch (start us, length us, event | category | flops | bytes accessed | tf_op | source)
XLA Modules:
  0.0 51.2 jit_solution(6613952753173470394)
XLA Ops:
  0.6 47.3 %shard_map.50 = (bf16[32,128,128]{2,1,0:T(8,128)(2,1)}, f32[8,128,128]{2,1,0:T(8,128)}) custom-call(s32[64]{0:T(128)} %slots_ref.1, f32[32,128,128]{2,1,0:T(8,128)} %bitcast.1, f32[8,128,128]{2,1,0:T(8,128)} %mom_ref.1), custom_call_target="tpu_custom_call" | custom-call | tf_op jit(solution)/shard_map/pallas_call | solution.py:373
  48.0 0.0 copy-start
  48.0 2.4 %copy.7 = bf16[32,128,128]{2,1,0:T(8,128)(2,1)} copy(bf16[32,128,128]{2,1,0:T(8,128)(2,1)} %get-tuple-element.4) | data formatting | bytes 2097152
  50.4 0.0 copy-done
  50.4 0.8 %copy.8 = f32[8,128,128]{2,1,0:T(8,128)} copy(f32[8,128,128]{2,1,0:T(8,128)S(1)} %copy-done) | data formatting | bytes 1048576
Async XLA Ops:
  48.0 2.4 %copy-start = (f32[8,128,128]{2,1,0:T(8,128)S(1)}, f32[8,128,128]{2,1,0:T(8,128)}, u32[]{:S(2)}) copy-start(f32[8,128,128]{2,1,0:T(8,128)} %get-tuple-element.5) | copy-start | bytes 1572868

commit v2 on v1

v2 whole, which is shorter than its diff:
```python
import functools
import math

import jax
import jax.numpy as jnp
from jax import lax
from jax.experimental import pallas as pl
from jax.experimental.pallas import tpu as pltpu
from jax.sharding import PartitionSpec as P

ITERS = 5

momentum_rate = 0.95
epsilon_norm = 1e-07
first_coef = 3.4445
third_coef = -4.775
fifth_coef = 2.0315

MESH = pl.DeviceIdType.MESH
F32 = jnp.float32
BF16 = jnp.bfloat16


def low_bit(d):
    return (d & -d).bit_length() - 1


def poly_of(iterate):
    gram = lax.dot_general(
        iterate, iterate, (((0,), (0,)), ((), ())), preferred_element_type=F32
    ).astype(BF16)
    square = jnp.dot(gram, gram, preferred_element_type=F32)
    return (third_coef * gram.astype(F32) + fifth_coef * square).astype(BF16)


def kernel(
    n_dp, n_ow, per, workers, pieces,
    slots_hbm, grads_hbm, mom_hbm, upd_ref, momout_ref,
    slots_ref, grads_ref, mom_ref, ypack, yrecv, zsend, zrecv, held, orecv, work, scale_ref, pall,
    slotss, gs, moms, ys, yr, zs, zr, os_, or_, ms, mr, as_, ar, pzs, pzr, pys, pyr, pxs, pxr, pcs, pcr,
):
    n_z = n_dp // 2
    n_x = n_ow // 2
    bits = n_z.bit_length() - 1
    mats = grads_ref.shape[0]
    rows = grads_ref.shape[1]
    cols = grads_ref.shape[2]
    full = n_ow * rows
    nb = mats // n_dp
    each = nb // pieces
    n_slots = mom_ref.shape[0]
    dp = lax.axis_index("dp")
    ow = lax.axis_index("owner")
    z = lax.div(dp, 2)
    y = lax.rem(dp, 2)
    x = lax.div(ow, 2)
    core = lax.rem(ow, 2)
    other = 2 * z + 1 - y
    sibling = 2 * x + 1 - core

    def flip(d):
        out = z
        for i in range(bits):
            if (d >> i) & 1:
                out = out + (1 << i) * (1 - 2 * lax.rem(lax.div(z, 1 << i), 2))
        return out

    def lane_from(t):
        return 2 * lax.rem(x - t + n_x, n_x) + core

    def lane_at(t):
        return 2 * lax.rem(x + t, n_x) + core

    def twin_from(t):
        return 2 * lax.rem(x - t + n_x, n_x) + 1 - core

    def member(d, s):
        return 2 * flip(d) + (y if s == 0 else 1 - y)

    def remote(src, dst, send, recv, to):
        return pltpu.make_async_remote_copy(
            src_ref=src, dst_ref=dst, send_sem=send, recv_sem=recv,
            device_id=to, device_id_type=MESH,
        )

    def only(cond, fn):
        if cond is None:
            fn()
        else:
            pl.when(cond)(fn)

    def works(lane):
        return None if workers == n_ow else lane < workers

    sent = []

    def launch(copy, cond=None):
        only(cond, copy.start)
        sent.append((copy, cond))

    barrier = pltpu.get_barrier_semaphore()

    def greet(member_id, lane):
        pl.semaphore_signal(barrier, inc=1, device_id=(member_id, lane), device_id_type=MESH)

    for d in range(1, n_z):
        greet(member(d, 0), ow)
    greet(other, ow)
    for t in range(1, n_ow):
        greet(dp, lax.rem(ow + t, n_ow))
    diagonal = tuple(range(FIRST_DIAG, n_z))
    for t in range(1, n_x if diagonal else 1):
        greet(other, lane_at(t))
    greeted = (n_z - 1) + 1 + (n_ow - 1) + (n_x - 1 if diagonal else 0)

    slots_copy = pltpu.make_async_copy(slots_hbm, slots_ref, slotss)
    slots_copy.start()
    mom_copy = pltpu.make_async_copy(mom_hbm, mom_ref, moms)
    mom_copy.start()

    def grads_copy(d, s):
        where = pl.ds(member(d, s) * nb, nb)
        return pltpu.make_async_copy(grads_hbm.at[where], grads_ref.at[where], gs.at[d, s])

    for s in (1, 0):
        for d in reversed(range(n_z)):
            grads_copy(d, s).start()

    slots_copy.wait()
    held_slots = [slots_ref[dp * n_slots + k] for k in range(n_slots)]

    def partial(m):
        place = jnp.int32(0)
        weight = F32(0.0)
        for k in range(n_slots):
            hit = held_slots[k] == m
            place = jnp.where(hit, k, place)
            weight = jnp.where(hit, F32(momentum_rate), weight)
        return grads_ref[m] + weight * mom_ref[place]

    mom_copy.wait()
    y_copies = {}
    for d in reversed(range(n_z)):
        grads_copy(d, 1).wait()
        for q in range(pieces):
            def pack(j, carry, d=d, q=q):
                b = q * each + j
                ypack[d, b] = partial(member(d, 1) * nb + b).astype(BF16)
                return carry
            lax.fori_loop(0, each, pack, 0)
            if d == n_z - 1 and q == 0:
                pl.semaphore_wait(barrier, greeted)
            part = pl.ds(q * each, each)
            y_copies[d, q] = remote(
                ypack.at[d, part], yrecv.at[d, part], ys.at[d, q], yr.at[d, q], (other, ow))
            launch(y_copies[d, q])
    for d in reversed(range(n_z)):
        grads_copy(d, 0).wait()

    def z_copy(d, q):
        part = pl.ds(q * each, each)
        return remote(
            zsend.at[d - 1, part], zrecv.at[d - 1, part], zs.at[d - 1, q], zr.at[d - 1, q],
            (member(1 << low_bit(d), 0), ow))

    def o_copy(b):
        return remote(
            held.at[pl.ds(dp * nb + b, 1)], orecv.at[ow, pl.ds(b % per, 1)],
            os_.at[b], or_.at[ow, b % per], (dp, b // per))

    def o_arrival(o, p):
        here = orecv.at[o, pl.ds(p, 1)]
        return remote(here, here, os_.at[p], or_.at[o, p], (dp, o))

    def m_copy(d, q):
        where = pl.ds(member(d & (d - 1), 0) * nb + q * each, each)
        there = held.at[where]
        return remote(
            there, there, ms.at[d - 1, q], mr.at[d - 1, q], (member(1 << low_bit(d), 0), ow))

    def m_arrival(d, q):
        where = pl.ds(member(d, 0) * nb + q * each, each)
        here = held.at[where]
        return remote(
            here, here, ms.at[d - 1, q], mr.at[d - 1, q], (member(1 << low_bit(d), 0), ow))

    def across(d, q, s=0):
        where = pl.ds(member(d, s) * nb + q * each, each)
        piece = held.at[where]
        return remote(piece, piece, as_.at[d, q], ar.at[d, q], (other, ow))

    def m_spread(d, q):
        for i in range(low_bit(d) if d else bits):
            launch(m_copy(d + (1 << i), q))
        launch(across(d, q))

    def m_pass(d, q):
        m_arrival(d, q).wait_recv()
        m_spread(d, q)

    for d in reversed(range(n_z)):
        steps = low_bit(d) if d else bits
        for q in range(pieces):
            y_copies[d, q].wait_recv()
            for i in range(steps):
                z_copy(d + (1 << i), q).wait_recv()

            def add(j, carry, d=d, q=q, steps=steps):
                b = q * each + j
                value = partial(member(d, 0) * nb + b) + yrecv[d, b].astype(F32)
                for i in range(steps):
                    value = value + zrecv[d + (1 << i) - 1, b].astype(F32)
                if d:
                    zsend[d - 1, b] = value.astype(BF16)
                else:
                    held[dp * nb + b] = value.astype(BF16)
                return carry
            lax.fori_loop(0, each, add, 0)
            if d:
                launch(z_copy(d, q))
            else:
                for b in range(q * each, (q + 1) * each):
                    launch(o_copy(b), ow != b // per)
                m_spread(0, q)

    passes = [(d, q) for d in range(1, n_z) for q in range(pieces)]

    def some(count):
        for _ in range(min(count, len(passes))):
            m_pass(*passes.pop(0))

    def begin():
        for p in range(per):
            orecv[ow, p] = held[dp * nb + ow * per + p]
            for o in range(n_ow):
                pl.when(ow != o)(o_arrival(o, p).wait_recv)
        for p in range(per):
            block = jnp.concatenate([orecv[o, p].astype(F32) for o in range(n_ow)], axis=0)
            norm = jnp.sqrt(jnp.sum(block * block, axis=(0, 1), keepdims=True)) + epsilon_norm
            iterate = (block / norm).astype(BF16)
            scale_ref[p] = jnp.broadcast_to(math.sqrt(full) / norm, scale_ref.shape[1:])
            poly = poly_of(iterate)
            advanced = first_coef * iterate.astype(F32) + jnp.dot(
                iterate, poly, preferred_element_type=F32)
            work[p, pl.ds(0, full)] = advanced.astype(BF16)
            at_row = lax.broadcasted_iota(jnp.int32, (cols, cols), 0)
            at_col = lax.broadcasted_iota(jnp.int32, (cols, cols), 1)
            eye = jnp.where(at_row == at_col, F32(first_coef), F32(0.0))
            work[p, pl.ds(full, cols)] = (eye + poly.astype(F32)).astype(BF16)

    def sweep():
        for p in range(per):
            both = work[p]
            poly = poly_of(both[:full])
            work[p] = (first_coef * both.astype(F32) + jnp.dot(
                both, poly, preferred_element_type=F32)).astype(BF16)

    def end():
        for p in range(per):
            poly = poly_of(work[p, pl.ds(0, full)])
            factor = work[p, pl.ds(full, cols)]
            last = first_coef * factor.astype(F32) + jnp.dot(
                factor, poly, preferred_element_type=F32)
            pall[dp * nb + ow * per + p] = (scale_ref[p, 0:1] * last).astype(BF16)

    some(PRE)
    only(works(ow), begin)
    for _ in range(ITERS - 2):
        some(MID)
        only(works(ow), sweep)
    some(MID)
    only(works(ow), end)

    def unit(d, s, lane):
        return pall.at[pl.ds(member(d, s) * nb + lane * per, per)]

    def pz_copy(d, arrival=False):
        there = unit(d if arrival else 0, 0, ow)
        return remote(there, there, pzs.at[d - 1], pzr.at[d - 1], (member(d, 0), ow))

    def py_copy(d, s=0):
        there = unit(d, s, ow)
        return remote(there, there, pys.at[d], pyr.at[d], (other, ow))

    def px_copy(d, s, t, arrival=False):
        there = unit(d, s, lane_from(t) if arrival else ow)
        return remote(there, there, pxs.at[t - 1, d, s], pxr.at[t - 1, d, s], (dp, lane_at(t)))

    def pc_copy(d, s, t, arrival=False):
        there = unit(d, s, twin_from(t) if arrival else lane_from(t))
        return remote(there, there, pcs.at[t, d, s], pcr.at[t, d, s], (dp, sibling))

    def pd_copy(d, t, arrival=False):
        there = unit(d, 1 if arrival else 0, lane_from(t) if arrival else ow)
        return remote(
            there, there, pxs.at[t - 1, d, 1], pxr.at[t - 1, d, 1], (other, lane_at(t)))

    def emit(d, s):
        for t in range(1, n_x):
            if not (s and d in diagonal):
                launch(px_copy(d, s, t), works(ow))
            if not s and d in diagonal:
                launch(pd_copy(d, t), works(ow))
        launch(pc_copy(d, s, 0), works(ow))

    def at_y(d):
        only(works(ow), py_copy(d, 1).wait_recv)
        emit(d, 1)

    def at_z(d):
        only(works(ow), pz_copy(d, True).wait_recv)
        launch(py_copy(d), works(ow))
        emit(d, 0)

    def at_x(d, s):
        for t in range(1, n_x):
            lane = lane_from(t)
            arrived = pd_copy(d, t, True) if s and d in diagonal else px_copy(d, s, t, True)
            only(works(lane), arrived.wait_recv)
            launch(pc_copy(d, s, t), works(lane))

    landed = set()

    def far_rows(d):
        if d not in landed:
            landed.add(d)
            for q in range(pieces):
                across(d, q, 1).wait_recv()

    def form(d, s):
        for t in range(n_x):
            only(works(twin_from(t)), pc_copy(d, s, t, True).wait_recv)
        if s:
            far_rows(d)
        first = member(d, s) * nb
        for b in range(nb):
            upd_ref[first + b] = jnp.dot(
                held[first + b], pall[first + b], preferred_element_type=F32).astype(BF16)

    def renew():
        for d in range(n_z):
            far_rows(d)

        def one(k, carry):
            m = slots_ref[dp * n_slots + k]
            present = jnp.where(m >= 0, F32(1.0), F32(0.0))
            momout_ref[k] = present * held[jnp.maximum(m, 0)].astype(F32) + (
                1.0 - present) * (F32(momentum_rate) * mom_ref[k])
            return carry
        lax.fori_loop(0, n_slots, one, 0)

    for d in reversed(range(1, n_z)):
        launch(pz_copy(d), works(ow))
    launch(py_copy(0), works(ow))
    emit(0, 0)
    some(len(passes) - LATE * pieces)
    at_y(0)
    at_x(0, 0)
    for d in range(1, n_z):
        at_z(d)
    some(len(passes))
    at_x(0, 1)
    formed = [(0, 0), (0, 1)] + [(d, 0) for d in range(1, n_z)] + [(d, 1) for d in range(1, n_z)]
    for d in range(1, n_z):
        at_y(d)
        at_x(d, 0)
        form(*formed.pop(0))
    for d in range(1, n_z):
        form(*formed.pop(0))
        if d == n_z - 1:
            renew()
        at_x(d, 1)
    while formed:
        form(*formed.pop(0))

    for copy, cond in sent:
        only(cond, copy.wait_send)


def writer(upd_ref, mom_ref, upd_hbm, mom_hbm, sems):
    parts = sems.shape[0] // 2
    copies = []
    for i, (src, dst) in enumerate(((upd_ref, upd_hbm), (mom_ref, mom_hbm))):
        count = src.shape[0] // parts
        for q in range(parts):
            where = pl.ds(q * count, count)
            copies.append(pltpu.make_async_copy(src.at[where], dst.at[where], sems.at[i * parts + q]))
    for copy in copies:
        copy.start()
    for copy in copies:
        copy.wait()


PRE, MID, LATE = 2, 1, 1
FIRST_DIAG = 99


def local(n_dp, n_ow, grads, momentum, slot_matrix):
    mats, rows, cols = grads.shape[1:]
    n_slots = momentum.shape[0]
    nb = mats // n_dp
    n_z = n_dp // 2
    n_x = n_ow // 2
    workers = min(nb, n_ow)
    per = nb // workers
    pieces = max(1, min(nb, 4 * nb // n_z))
    block = (rows, cols)
    vmem = pl.BlockSpec(memory_space=pltpu.VMEM)
    hbm = pl.BlockSpec(memory_space=pltpu.HBM)
    dma = pltpu.SemaphoreType.DMA
    hops = n_z - 1
    counts = (
        (n_z, pieces), (hops, pieces), None, (hops, pieces), (n_z, pieces),
        (hops,), (n_z,), (n_x - 1, n_z, 2), (n_x, n_z, 2),
    )
    sems = [dma, dma((n_z, 2)), dma]
    for count in counts:
        sems += [dma(count)] * 2 if count else [dma((nb,)), dma((n_ow, per))]
    own_grads = pltpu.with_memory_space_constraint(grads[0], pltpu.HBM)
    own_slots = pltpu.with_memory_space_constraint(slot_matrix, pltpu.HBM)
    own_momentum = pltpu.with_memory_space_constraint(momentum, pltpu.HBM)
    updates, renewed = pl.pallas_call(
        functools.partial(kernel, n_dp, n_ow, per, workers, pieces),
        out_shape=(
            pltpu.VMEM((mats,) + block, BF16),
            pltpu.VMEM(momentum.shape, F32),
        ),
        in_specs=[hbm, hbm, hbm],
        out_specs=(vmem, vmem),
        scratch_shapes=[
            pltpu.SMEM(slot_matrix.shape, jnp.int32),
            pltpu.VMEM((mats,) + block, F32),
            pltpu.VMEM((n_slots,) + block, F32),
            pltpu.VMEM((n_z, nb) + block, BF16),
            pltpu.VMEM((n_z, nb) + block, BF16),
            pltpu.VMEM((hops, nb) + block, BF16),
            pltpu.VMEM((hops, nb) + block, BF16),
            pltpu.VMEM((mats,) + block, BF16),
            pltpu.VMEM((n_ow, per) + block, BF16),
            pltpu.VMEM((per, n_ow * rows + cols, cols), BF16),
            pltpu.VMEM((per, 8, cols), F32),
            pltpu.VMEM((mats, cols, cols), BF16),
        ] + sems,
        compiler_params=pltpu.CompilerParams(
            collective_id=0, has_side_effects=True, vmem_limit_bytes=40 * 2**20),
    )(own_slots, own_grads, own_momentum)
    return pl.pallas_call(
        writer,
        out_shape=(
            jax.ShapeDtypeStruct((mats,) + block, BF16),
            jax.ShapeDtypeStruct(momentum.shape, F32),
        ),
        in_specs=[vmem, vmem],
        out_specs=(hbm, hbm),
        scratch_shapes=[dma((8,))],
        compiler_params=pltpu.CompilerParams(vmem_limit_bytes=40 * 2**20),
    )(updates, renewed)


def solution(mesh):
    return jax.shard_map(
        functools.partial(local, mesh.shape["dp"], mesh.shape["owner"]),
        mesh=mesh,
        in_specs=(P("dp", None, "owner", None), P("dp", "owner", None), P()),
        out_specs=(P(None, "owner", None), P("dp", "owner", None)),
        check_vma=False,
    )
```

time: 51.7 us -> 43.3 us (0.84)
  Pallas kernels: 47.3 us -> 42.5 us
  local copies, waits for them, and re-layouts: 3.16 us -> 0 us
    pallas_call x1, Pallas kernels: 47.3 us -> 41.3 us  [local(): pl.pallas_call(functools.partial(kernel, n_dp, n_ow, per, workers, pieces...]
    unnamed x4 -> x0, local copies, waits for them, and re-layouts: 3.16 us -> none
    pallas_call x0 -> x1, Pallas kernels: none -> 1.2 us  [local(): pl.pallas_call(writer, out_shape=(jax.ShapeDtypeStruct((mats,) + block, B...]
where the time goes in v2:
time: 43.3 us; the launch traced here: 43.1 us
  Pallas kernels  42.5 us (98%)
  between operations  0.64 us (1%)
    pallas_call x1, Pallas kernels, local(): pl.pallas_call(functools.partial(kernel, n_dp, n_ow, per, workers, pieces...  41.3 us
    pallas_call x1, Pallas kernels, local(): pl.pallas_call(writer, out_shape=(jax.ShapeDtypeStruct((mats,) + block, B...  1.2 us

profile of v2, /device:TPU:0, one launch (start us, length us, event | category | flops | bytes accessed | tf_op | source)
XLA Modules:
  0.0 43.1 jit_solution(10174023295588162637)
XLA Ops:
  0.6 41.3 %shard_map.50 = (bf16[32,128,128]{2,1,0:T(8,128)(2,1)S(1)}, f32[8,128,128]{2,1,0:T(8,128)S(1)}) custom-call(s32[64]{0:T(128)} %slots_hbm.1, f32[32,128,128]{2,1,0:T(8,128)} %bitcast.1, f32[8,128,128]{2,1,0:T(8,128)} %mom_hbm.1), custom_call_target="tpu_custom_call" | custom-call | tf_op jit(solution)/shard_map/pallas_call | solution.py:422
  41.9 1.2 %shard_map.51 = (bf16[32,128,128]{2,1,0:T(8,128)(2,1)}, f32[8,128,128]{2,1,0:T(8,128)}) custom-call(bf16[32,128,128]{2,1,0:T(8,128)(2,1)S(1)} %get-tuple-element.4.upd_ref, f32[8,128,128]{2,1,0:T(8,128)S(1)} %get-tuple-element.5.mom_ref), custom_call_target="tpu_custom_call" | custom-call | tf_op jit(solution)/shard_map/pallas_call | solution.py:447
